TPU v7x, 32 devices: a whole 2x2x4 slice. The times are simulated.
32 devices in a mesh: gx: 4 (over z), wa: 8 (over y, x, core).
Axes of the slice: x: 2, y: 2, z: 4, core: 2. Of those that a mesh axis runs over, the one named last changes fastest.
Arguments:
- positions: float32 [512, 3, 256], P(('gx', 'wa')), may hold values from 0 to 1
- weights: float32 [512, 256], P(('gx', 'wa')), may hold values from 0.5 to 2
- block_count: int32 [512], P(('gx', 'wa')), may hold values from 1 to 256
- send_list: int32 [32, 8, 2], P(('gx', 'wa')), may hold values from 0 to 15
- unit_pair: int32 [32, 16], P(('gx', 'wa')), may hold values from 0 to 15, each once within a row
- unit_live: int32 [32], P(('gx', 'wa')), may hold values from 2 to 16, as said below
Outputs:
- slab_counts: float32 [4, 30, 20], P('gx')
- totals: float32 [30, 20], replicated
Inputs may be any that keep to these rules, and one draw needn't show every extreme that they name: `unit_pair`: each row holds every slot number once. `unit_live`: the active units of a device are the first ones of its list; some device has all 16 active.
All inputs are finite; a program needn't handle non-finite values.
Results may differ from a plain program's by a relative error of at most 0.0003.
Values sent between devices are 32-bit elements; how exact they have to be, the bound alone decides.
No kernel may reach another device: no remote copies, remote signals or barrier semaphores. Data moves between devices by JAX's collectives and lax.ppermute only.
A program may use at most 64 MiB of HBM per device.

v0:
```python
import jax
import jax.numpy as jnp
from jax import lax
from jax.sharding import PartitionSpec as P

SBINS = 30
MUBINS = 20


reach = 0.5
viewer = (0.5, 0.5, -1.5)
units_per_turn = 4


def passed_along(shard, axis, by):
    count = lax.axis_size(axis)
    return lax.ppermute(shard, axis, [(i, (i + by) % count) for i in range(count)])


def group_counts(a_pos, a_wgt, b_pos, b_wgt):
    step = reach / SBINS
    diff = a_pos[:, :, :, None] - b_pos[:, :, None, :]
    eye_at = jnp.array(viewer, dtype=jnp.float32)[None, :, None, None]
    middle = 0.5 * (a_pos[:, :, :, None] + b_pos[:, :, None, :]) + eye_at
    square = jnp.sum(diff * diff, axis=1)
    dist = jnp.sqrt(square)
    along = jnp.abs(jnp.sum(diff * middle, axis=1)) / jnp.sqrt(
        jnp.maximum(square, step * step) * jnp.sum(middle * middle, axis=1)
    )
    s_mid = jnp.arange(SBINS, dtype=jnp.float32) + 0.5
    m_mid = jnp.arange(MUBINS, dtype=jnp.float32) + 0.5
    s_hat = jnp.maximum(
        0.0, 1.0 - jnp.abs(dist[:, None] / step - s_mid[None, :, None, None])
    ).astype(jnp.bfloat16)
    pair_w = a_wgt[:, :, None] * b_wgt[:, None, :]
    m_hat = (
        jnp.maximum(0.0, 1.0 - jnp.abs(along[:, None] * MUBINS - m_mid[None, :, None, None]))
        * pair_w[:, None]
    ).astype(jnp.bfloat16)
    return jnp.einsum("gkab,gjab->kj", s_hat, m_hat, preferred_element_type=jnp.float32)


def per_device(positions, weights, block_count, send_list, unit_pair, unit_live):
    block = positions.shape[2]
    per_peer = send_list.shape[2]
    peers = lax.axis_size("wa")
    units = peers * per_peer
    live = jnp.arange(block, dtype=jnp.int32)[None, :] < block_count[:, None]
    masked = jnp.where(live, weights, jnp.float32(0.0))
    picks = send_list[0].reshape(-1)
    send_pos = positions[picks].reshape(peers, per_peer, 3, block)
    send_wgt = masked[picks].reshape(peers, per_peer, block)
    own_pos, own_wgt = (
        lax.all_to_all(send_pos, "wa", split_axis=0, concat_axis=0, tiled=True),
        lax.all_to_all(send_wgt, "wa", split_axis=0, concat_axis=0, tiled=True),
    )
    below_pos, below_wgt = passed_along((own_pos, own_wgt), "gx", 1)
    own_pos = own_pos.reshape(units, 3, block)
    own_wgt = own_wgt.reshape(units, block)
    below_pos = below_pos.reshape(units, 3, block)
    below_wgt = below_wgt.reshape(units, block)
    partner = unit_pair[0]
    partner_pos = below_pos[partner]
    partner_wgt = below_wgt[partner]
    active = jnp.arange(units, dtype=jnp.int32) < unit_live[0]
    own_wgt = jnp.where(active[:, None], own_wgt, jnp.float32(0.0))
    start = jnp.zeros((SBINS, MUBINS), jnp.float32)
    turns = units // units_per_turn
    items = (
        own_pos.reshape(turns, units_per_turn, 3, block),
        own_wgt.reshape(turns, units_per_turn, block),
        partner_pos.reshape(turns, units_per_turn, 3, block),
        partner_wgt.reshape(turns, units_per_turn, block),
    )

    def accumulate(total, group):
        return (total + group_counts(*group), None)

    total, _ = lax.scan(accumulate, start, items)
    scale = 10.0 * SBINS * MUBINS / (peers * units * block * block)
    slab = lax.psum(total, "wa") * scale
    whole = lax.psum(slab, "gx") / lax.axis_size("gx")
    return (slab[None], whole)


def solution(mesh):
    return jax.shard_map(
        per_device,
        mesh=mesh,
        in_specs=(
            P(("gx", "wa"), None, None),
            P(("gx", "wa"), None),
            P(("gx", "wa")),
            P(("gx", "wa"), None, None),
            P(("gx", "wa"), None),
            P(("gx", "wa")),
        ),
        out_specs=(P("gx", None, None), P()),
        check_vma=False,
    )
```

profile of v0, /device:TPU:0, one launch (start us, length us, event | category | flops | bytes accessed | tf_op | source)
XLA Modules:
  0.0 132.2 jit_solution(15789836194075726807)
XLA Ops:
  0.7 0.8 copy.30
  1.5 0.8 fusion.12
  2.3 0.6 gather_fusion.2
  2.9 0.6 reshape.132
  3.5 5.2 %all-to-all-start.1 = ((f32[8,2,256]{2,1,0:T(2,128)}), f32[8,2,256]{2,1,0:T(2,128)S(1)}, u32[]{:S(2)}, u32[]{:S(2)}) async-start(f32[8,2,256]{2,1,0:T(2,128)} %reshape.132), calls=%async_computation.1 | async-start | bytes 32768 | tf_op jit(solution)/shard_map/all_to_all | solution.py:55
  8.7 0.7 fusion.14
  9.4 0.6 gather_fusion
  10.0 0.6 copy.31
  11.3 2.1 %all-to-all-done.1 = f32[8,2,256]{2,1,0:T(2,128)S(1)} async-done(((f32[8,2,256]{2,1,0:T(2,128)}), f32[8,2,256]{2,1,0:T(2,128)S(1)}, u32[]{:S(2)}, u32[]{:S(2)}) %all-to-all-start.1) | async-done | bytes 16416 | tf_op jit(solution)/shard_map/all_to_all | solution.py:55
  13.5 3.3 %all-to-all-start = ((f32[8,2,3,256]{3,1,2,0:T(2,128)}), f32[8,2,3,256]{3,1,2,0:T(2,128)S(1)}, u32[]{:S(2)}, u32[]{:S(2)}) async-start(f32[8,2,3,256]{3,1,2,0:T(2,128)} %copy.31), calls=%async_computation | async-start | bytes 98304 | tf_op jit(solution)/shard_map/all_to_all | solution.py:54
  16.8 1.6 %collective-permute-start.1 = (f32[8,2,256]{2,1,0:T(2,128)S(1)}, f32[8,2,256]{2,1,0:T(2,128)S(1)}, u32[]{:S(2)}, u32[]{:S(2)}) collective-permute-start(f32[8,2,256]{2,1,0:T(2,128)S(1)} %all-to-all-done.1), channel_id=1, source_target_pairs={{0,8},{8,16},{16,24},{24,0},{1,9},{9,17},{17,25},{25,1},{2,10},{10... | collective-permute-start | bytes 49160 | tf_op jit(solution)/shard_map/ppermute | solution.py:17
  18.5 3.2 %all-to-all-done = f32[8,2,3,256]{3,1,2,0:T(2,128)S(1)} async-done(((f32[8,2,3,256]{3,1,2,0:T(2,128)}), f32[8,2,3,256]{3,1,2,0:T(2,128)S(1)}, u32[]{:S(2)}, u32[]{:S(2)}) %all-to-all-start) | async-done | bytes 49184 | tf_op jit(solution)/shard_map/all_to_all | solution.py:54
  21.7 1.6 %collective-permute-start = (f32[8,2,3,256]{3,1,2,0:T(2,128)S(1)}, f32[8,2,3,256]{3,1,2,0:T(2,128)S(1)}, u32[]{:S(2)}, u32[]{:S(2)}) collective-permute-start(f32[8,2,3,256]{3,1,2,0:T(2,128)S(1)} %all-to-all-done), channel_id=1, source_target_pairs={{0,8},{8,16},{16,24},{24,0},{1,9},{9,17},{17,25},{25,1},{2,10},{10... | collective-permute-start | bytes 147464 | tf_op jit(solution)/shard_map/ppermute | solution.py:17
  23.4 0.6 gather_fusion.3
  24.0 3.6 %collective-permute-done = f32[8,2,3,256]{3,1,2,0:T(2,128)S(1)} collective-permute-done((f32[8,2,3,256]{3,1,2,0:T(2,128)S(1)}, f32[8,2,3,256]{3,1,2,0:T(2,128)S(1)}, u32[]{:S(2)}, u32[]{:S(2)}) %collective-permute-start) | collective-permute-done | bytes 49184 | tf_op jit(solution)/shard_map/ppermute | solution.py:17
  27.6 0.6 gather_fusion.1
  28.2 63.3 %while.12 = (s32[]{:T(128)}, f32[30,20]{0,1:T(8,128)S(1)}, f32[4,4,3,256]{3,2,1,0:T(4,128)S(1)}, f32[4,4,3,256]{3,2,1,0:T(4,128)S(1)}, f32[4,4,256]{2,1,0:T(4,12...) while((s32[]{:T(128)}, f32[30,20]{0,1:T(8,128)S(1)}, ...), condition=%wide.region_4.5_spmd.clone.clone, body=%wide.region_0.4_spmd.sunk.clone.clone.sunk | while | flops 394265856 | bytes 16889040 | solution.py:79
  28.2 1.4 %fusion.17 = (f32[4,256,256]{2,1,0:T(8,128)S(1)}, f32[4,256,256]{2,1,0:T(8,128)S(1)}, f32[4,256,256]{2,1,0:T(8,128)S(1)}) fusion(f32[3]{0:T(128)S(1)} %get-tuple-element.207, f32[4,3,256]{2,1,0:T(4,128)S(1)} %get-tuple-element.175, f32[4,3,256]{2,1,0:T(4,128)S(1)} %get-tuple-element.176), kind=kLoop, calls=%fused_computation.15.clone.1 | loop fusion | flops 7077888 | bytes 3170316 | tf_op jit(solution)/shard_map/while/body/eval_jaxpr/reduce_sum | solution.py:27
  29.7 0.5 sqrt_multiply_fusion.2
  30.2 0.7 copy.44
  30.8 0.7 copy.45
  31.5 0.1 copy.43
  31.7 0.3 broadcast_multiply_fusion.4
  32.1 11.9 %fusion.18 = f32[30,20]{0,1:T(8,128)S(1)} fusion(f32[4,256,256]{2,0,1:T(4,128)S(1)} %broadcast_multiply_fusion.4, f32[20]{0:T(128)S(1)} %iota_add_fusion.4, f32[4,256,256]{2,0,1:T(4,128)S(1)} %copy.44, f32[30]{0:T(128)S(1)} %iota_add_fusion.5, f32[4,256,256]{2,0,1:T(4,128)S(1)} %copy.45, f32[30,20]{0,1:T(8,128)S(1)} %get-tuple-element.192, ...), kind=kOutput, calls=%fused_computation.19.clone.1 | convolution fusion | flops 385352896 | bytes 3150729 | tf_op jit(solution)/shard_map/while/body/eval_jaxpr/gkab,gjab->kj/dot_general | solution.py:40
  44.1 1.4 %fusion.17 = (f32[4,256,256]{2,1,0:T(8,128)S(1)}, f32[4,256,256]{2,1,0:T(8,128)S(1)}, f32[4,256,256]{2,1,0:T(8,128)S(1)}) fusion(f32[3]{0:T(128)S(1)} %get-tuple-element.207, f32[4,3,256]{2,1,0:T(4,128)S(1)} %get-tuple-element.175, f32[4,3,256]{2,1,0:T(4,128)S(1)} %get-tuple-element.176), kind=kLoop, calls=%fused_computation.15.clone.1 | loop fusion | flops 7077888 | bytes 3170316 | tf_op jit(solution)/shard_map/while/body/eval_jaxpr/reduce_sum | solution.py:27
  45.5 0.5 sqrt_multiply_fusion.2
  46.0 0.7 copy.44
  46.7 0.7 copy.45
  47.4 0.1 copy.43
  47.5 0.3 broadcast_multiply_fusion.4
  47.9 11.9 %fusion.18 = f32[30,20]{0,1:T(8,128)S(1)} fusion(f32[4,256,256]{2,0,1:T(4,128)S(1)} %broadcast_multiply_fusion.4, f32[20]{0:T(128)S(1)} %iota_add_fusion.4, f32[4,256,256]{2,0,1:T(4,128)S(1)} %copy.44, f32[30]{0:T(128)S(1)} %iota_add_fusion.5, f32[4,256,256]{2,0,1:T(4,128)S(1)} %copy.45, f32[30,20]{0,1:T(8,128)S(1)} %get-tuple-element.192, ...), kind=kOutput, calls=%fused_computation.19.clone.1 | convolution fusion | flops 385352896 | bytes 3150729 | tf_op jit(solution)/shard_map/while/body/eval_jaxpr/gkab,gjab->kj/dot_general | solution.py:40
  59.9 1.4 %fusion.17 = (f32[4,256,256]{2,1,0:T(8,128)S(1)}, f32[4,256,256]{2,1,0:T(8,128)S(1)}, f32[4,256,256]{2,1,0:T(8,128)S(1)}) fusion(f32[3]{0:T(128)S(1)} %get-tuple-element.207, f32[4,3,256]{2,1,0:T(4,128)S(1)} %get-tuple-element.175, f32[4,3,256]{2,1,0:T(4,128)S(1)} %get-tuple-element.176), kind=kLoop, calls=%fused_computation.15.clone.1 | loop fusion | flops 7077888 | bytes 3170316 | tf_op jit(solution)/shard_map/while/body/eval_jaxpr/reduce_sum | solution.py:27
  61.3 0.5 sqrt_multiply_fusion.2
  61.8 0.7 copy.44
  62.5 0.7 copy.45
  63.2 0.1 copy.43
  63.3 0.3 broadcast_multiply_fusion.4
  63.7 11.9 %fusion.18 = f32[30,20]{0,1:T(8,128)S(1)} fusion(f32[4,256,256]{2,0,1:T(4,128)S(1)} %broadcast_multiply_fusion.4, f32[20]{0:T(128)S(1)} %iota_add_fusion.4, f32[4,256,256]{2,0,1:T(4,128)S(1)} %copy.44, f32[30]{0:T(128)S(1)} %iota_add_fusion.5, f32[4,256,256]{2,0,1:T(4,128)S(1)} %copy.45, f32[30,20]{0,1:T(8,128)S(1)} %get-tuple-element.192, ...), kind=kOutput, calls=%fused_computation.19.clone.1 | convolution fusion | flops 385352896 | bytes 3150729 | tf_op jit(solution)/shard_map/while/body/eval_jaxpr/gkab,gjab->kj/dot_general | solution.py:40
  75.7 1.4 %fusion.17 = (f32[4,256,256]{2,1,0:T(8,128)S(1)}, f32[4,256,256]{2,1,0:T(8,128)S(1)}, f32[4,256,256]{2,1,0:T(8,128)S(1)}) fusion(f32[3]{0:T(128)S(1)} %get-tuple-element.207, f32[4,3,256]{2,1,0:T(4,128)S(1)} %get-tuple-element.175, f32[4,3,256]{2,1,0:T(4,128)S(1)} %get-tuple-element.176), kind=kLoop, calls=%fused_computation.15.clone.1 | loop fusion | flops 7077888 | bytes 3170316 | tf_op jit(solution)/shard_map/while/body/eval_jaxpr/reduce_sum | solution.py:27
  77.1 0.5 sqrt_multiply_fusion.2
  77.6 0.7 copy.44
  78.3 0.7 copy.45
  79.2 0.3 broadcast_multiply_fusion.4
  79.5 11.9 %fusion.18 = f32[30,20]{0,1:T(8,128)S(1)} fusion(f32[4,256,256]{2,0,1:T(4,128)S(1)} %broadcast_multiply_fusion.4, f32[20]{0:T(128)S(1)} %iota_add_fusion.4, f32[4,256,256]{2,0,1:T(4,128)S(1)} %copy.44, f32[30]{0:T(128)S(1)} %iota_add_fusion.5, f32[4,256,256]{2,0,1:T(4,128)S(1)} %copy.45, f32[30,20]{0,1:T(8,128)S(1)} %get-tuple-element.192, ...), kind=kOutput, calls=%fused_computation.19.clone.1 | convolution fusion | flops 385352896 | bytes 3150729 | tf_op jit(solution)/shard_map/while/body/eval_jaxpr/gkab,gjab->kj/dot_general | solution.py:40
  91.5 22.3 %psum.14 = f32[30,20]{0,1:T(8,128)S(1)} all-reduce(f32[30,20]{0,1:T(8,128)S(1)} %get-tuple-element.39), channel_id=1, replica_groups=mesh['gx'=4,'wa'=8] {'wa'}, use_global_device_ids=true, to_apply=%region_5.6 | all-reduce | flops 600 | bytes 4800 | tf_op jit(solution)/shard_map/psum | solution.py:81
  113.8 17.1 %psum.15 = f32[30,20]{0,1:T(8,128)S(1)} all-reduce(f32[30,20]{0,1:T(8,128)S(1)} %broadcast_multiply_fusion.2), channel_id=1, replica_groups=mesh['gx'=4,'wa'=8] {'gx'}, use_global_device_ids=true, to_apply=%region_6.7 | all-reduce | flops 600 | bytes 4800 | tf_op jit(solution)/shard_map/psum | solution.py:82
  130.9 0.6 broadcast_in_dim.24
  131.6 0.6 broadcast_multiply_fusion.1
  (40 shorter events, 0.6 us)
Async XLA Ops:
  0.6 8.8 %copy-start = (f32[16,3,256]{2,0,1:T(8,128)S(1)}, f32[16,3,256]{2,0,1:T(8,128)}, u32[]{:S(2)}) copy-start(f32[16,3,256]{2,0,1:T(8,128)} %param.9) | copy-start | bytes 147460
  0.6 27.5 %copy-start.1 = (f32[3]{0:T(128)S(1)}, f32[3]{0:T(128)}, u32[]{:S(2)}) copy-start(f32[3]{0:T(128)} %constant.46.clone..sunk.3) | copy-start | bytes 40
  3.5 10.0 %all-to-all-start.1 = ((f32[8,2,256]{2,1,0:T(2,128)}), f32[8,2,256]{2,1,0:T(2,128)S(1)}, u32[]{:S(2)}, u32[]{:S(2)}) async-start(f32[8,2,256]{2,1,0:T(2,128)} %reshape.132), calls=%async_computation.1 | async-start | bytes 32768 | tf_op jit(solution)/shard_map/all_to_all | solution.py:55
  13.5 8.2 %all-to-all-start = ((f32[8,2,3,256]{3,1,2,0:T(2,128)}), f32[8,2,3,256]{3,1,2,0:T(2,128)S(1)}, u32[]{:S(2)}, u32[]{:S(2)}) async-start(f32[8,2,3,256]{3,1,2,0:T(2,128)} %copy.31), calls=%async_computation | async-start | bytes 98304 | tf_op jit(solution)/shard_map/all_to_all | solution.py:54
  16.8 6.5 %collective-permute-start.1 = (f32[8,2,256]{2,1,0:T(2,128)S(1)}, f32[8,2,256]{2,1,0:T(2,128)S(1)}, u32[]{:S(2)}, u32[]{:S(2)}) collective-permute-start(f32[8,2,256]{2,1,0:T(2,128)S(1)} %all-to-all-done.1), channel_id=1, source_target_pairs={{0,8},{8,16},{16,24},{24,0},{1,9},{9,17},{17,25},{25,1},{2,10},{10... | collective-permute-start | bytes 49160 | tf_op jit(solution)/shard_map/ppermute | solution.py:17
  21.7 5.9 %collective-permute-start = (f32[8,2,3,256]{3,1,2,0:T(2,128)S(1)}, f32[8,2,3,256]{3,1,2,0:T(2,128)S(1)}, u32[]{:S(2)}, u32[]{:S(2)}) collective-permute-start(f32[8,2,3,256]{3,1,2,0:T(2,128)S(1)} %all-to-all-done), channel_id=1, source_target_pairs={{0,8},{8,16},{16,24},{24,0},{1,9},{9,17},{17,25},{25,1},{2,10},{10... | collective-permute-start | bytes 147464 | tf_op jit(solution)/shard_map/ppermute | solution.py:17
where the time goes:
time: 133 us; the launch traced here: 132 us
  matrix products  47.8 us (36%)
  blocking collectives  39.5 us (30%)
  starting transfers between devices  11.7 us (9%)
  local copies, waits for them, and re-layouts  11.3 us (8%)
  other arithmetic  11.2 us (8%)
  waiting for transfers between devices  8.92 us (7%)
  between operations  1.38 us (1%)
    dot_general x4, matrix products, group_counts(): jnp.einsum('gkab,gjab->kj', s_hat, m_hat, preferred_element_type=jnp.floa...  47.8 us
    psum x1, blocking collectives, per_device(): slab = lax.psum(total, 'wa') * scale  22.3 us
    psum x1, blocking collectives, per_device(): whole = lax.psum(slab, 'gx') / lax.axis_size('gx')  17.1 us
    reduce_sum x4, other arithmetic, group_counts(): jnp.sum(diff * middle, axis=1)  5.74 us
    all_to_all x1, starting transfers between devices, per_device(): lax.all_to_all(send_wgt, 'wa', split_axis=0, concat_axis=0, tiled=True)  5.2 us
    ppermute x2, waiting for transfers between devices, passed_along(): lax.ppermute(shard, axis, [(i, (i + by) % count) for i in range(count)])  3.6 us
    all_to_all x1, starting transfers between devices, per_device(): lax.all_to_all(send_pos, 'wa', split_axis=0, concat_axis=0, tiled=True)  3.35 us
    ppermute x2, starting transfers between devices, passed_along(): lax.ppermute(shard, axis, [(i, (i + by) % count) for i in range(count)])  3.21 us
  transfers between devices with their start and end apart: 4, of which 3 were waited for; matrix products, arithmetic and copies ran while one was open for 2% of the time, Pallas kernels for 0%

commit v1 on v0

v1 whole, which is shorter than its diff:
```python
import functools

import jax
import jax.numpy as jnp
from jax import lax
from jax.experimental import pallas as pl
from jax.experimental.pallas import tpu as pltpu
from jax.sharding import PartitionSpec as P

SBINS = 30
MUBINS = 20
REACH = 0.5
STEP = REACH / SBINS
SCALE = 0.5 / STEP
LANES = 128
ROWS = 8
SPAN = 32
SLOTS = 8


def pack_kernel(count_ref, send_ref, pos_ref, wgt_ref, out_ref):
    slots, _, block = out_ref.shape
    per_peer = send_ref.shape[2]
    lane = lax.broadcasted_iota(jnp.int32, (1, block), 1)
    for slot in range(slots):
        src = send_ref[0, slot // per_peer, slot % per_peer]
        count = count_ref[src]
        pos = pos_ref[src]
        wgt = jnp.where(lane < count, wgt_ref[pl.ds(src, 1), :], 0.0)
        mark = jnp.logical_and(lane == block - 1, count < block)
        out_ref[slot, 0:1, :] = jnp.where(mark, count.astype(jnp.float32), pos[0:1])
        out_ref[slot, 1:3, :] = pos[1:3]
        out_ref[slot, 3:4, :] = wgt


def spread(row):
    return jnp.broadcast_to(row, (ROWS, LANES))


def pair_kernel(
    out_scale, live_ref, pair_ref, own_ref, below_ref, out_ref,
    rowf, colf, sep_now, sep_next, ang_next, rowblk, lanblk, wide, steps, *accs
):
    units, _, block = own_ref.shape
    accs = (accs[:SLOTS], accs[SLOTS:])
    live = live_ref[0]
    third = 4.0 * SCALE * SCALE * 3.0

    def features(src_ref, u, b):
        x, y, z, w = (src_ref[u, i:i + 1, :] for i in range(4))
        alive = w > 0.0
        count = jnp.where(alive[:, block - 1:], float(block), x[:, block - 1:])
        x = jnp.where(alive, x, 0.5)
        n = (x - 0.5) * (x + 1.5) + (y - 0.5) * (y + 1.5) + (z - 0.5) * (z - 2.5)
        m = (2.0 * SCALE * SCALE) * n
        feats = jnp.concatenate(
            [SCALE * x, SCALE * y, SCALE * z, (10.0 * SCALE * SCALE) * n, m, w, m + third, w], axis=0
        )
        for half in range(block // LANES):
            rowf[b, half] = feats[:, half * LANES:(half + 1) * LANES]
        colf[b] = feats.T
        return count

    group = 4

    def prepare(i, carry):
        for k in range(group):
            u = i * group + k
            steps[u] = features(own_ref, u, u)[0, 0].astype(jnp.int32)
            wide[u] = features(below_ref, u, units + u)[0, 0].astype(jnp.int32)
        return carry

    lax.fori_loop(0, units // group, prepare, 0)

    def rounds(rows, lanes):
        return jnp.where(lanes > LANES, (rows + 2 * ROWS - 1) // (2 * ROWS), (rows + 4 * ROWS - 1) // (4 * ROWS))

    def plan(u, total):
        other = pair_ref[0, u]
        na, nb = steps[u], wide[other]
        straight, turned = rounds(na, nb), rounds(nb, na)
        turn = turned < straight
        rowblk[u] = jnp.where(turn, units + other, u)
        lanblk[u] = jnp.where(turn, u, units + other)
        n = jnp.where(turn, turned, straight)
        lanblk[units + u] = jnp.where(jnp.where(turn, na, nb) > LANES, 1, 0)
        steps[u] = n
        return total + n

    total = lax.fori_loop(0, live, plan, 0)

    def advance(state):
        u, t = state
        last = t + 1 >= steps[u]
        return jnp.where(last, jnp.minimum(u + 1, live - 1), u), jnp.where(last, 0, t + 1)

    def geometry(state):
        u, t = state
        rb, lb, wd = rowblk[u], lanblk[u], lanblk[units + u]
        sep, ang = [], []
        for j in range(4):
            a0 = pl.multiple_of(jnp.where(wd == 1, t * 16 + 8 * (j // 2), t * 32 + 8 * j), ROWS)
            half = wd * (j % 2)
            col = colf[rb, pl.ds(a0, ROWS), :]
            ax, ay, az, aq, am, aw = (spread(col[:, c:c + 1]) for c in range(6))
            bx, by, bz, bq, bw, bm = (spread(rowf[lb, half, c:c + 1, :]) for c in (0, 1, 2, 3, 5, 6))
            dx, dy, dz = ax - bx, ay - by, az - bz
            square = dx * dx + dy * dy + dz * dz
            y = square * lax.rsqrt(jnp.maximum(square, 1e-12)) + 0.25
            norm = jnp.maximum(square, 0.25) * ((am + bm) - square)
            z = jnp.abs(aq - bq) * lax.rsqrt(norm) + 0.25
            w = aw * bw
            near = jnp.round(y)
            off = jnp.abs(y - near)
            sep.append((jnp.floor(y), near, off, 0.5 - off))
            near = jnp.round(z)
            off = jnp.abs(z - near)
            ang.append((jnp.floor(z), near, off * w, (0.5 - off) * w))
        return sep, ang

    base = lax.broadcasted_iota(jnp.int32, (ROWS, LANES), 0).astype(jnp.float32)
    marks = (base, base + 8.0, base + 1.0, base + 9.0)

    def hats(ref, j, r):
        even, odd, on_even, on_odd = (spread(ref[j, q, r:r + 1, :]) for q in range(4))
        return [
            jnp.where(even == marks[0], on_even, 0.0), jnp.where(even == marks[1], on_even, 0.0),
            jnp.where(odd == marks[2], on_odd, 0.0), jnp.where(odd == marks[3], on_odd, 0.0),
        ]

    def tile(ref, m, r):
        left, right = hats(ref, 2 * m, r), hats(ref, 2 * m + 1, r)
        return jnp.concatenate([jnp.concatenate([a, b], axis=1) for a, b in zip(left, right)], axis=0)

    def put(ref, values):
        for j in range(4):
            for q in range(4):
                ref[j, q] = values[j][q]

    def push():
        for m in range(2):
            rhs = jnp.concatenate([tile(ang_next, m, r) for r in range(SLOTS)], axis=0)
            pltpu.matmul_push_rhs(rhs, staging_register=0, mxu_index=m, transpose=True)

    for m in range(2):
        for r in range(SLOTS):
            pltpu.matmul_pop(accs[m][r])

    first = (jnp.int32(0), jnp.int32(0))
    sep, ang = geometry(first)
    put(sep_now, sep)
    put(ang_next, ang)
    push()
    second = advance(first)
    sep, ang = geometry(second)
    put(sep_next, sep)
    put(ang_next, ang)

    def turn(_, state):
        for r in range(SLOTS):
            for m in range(2):
                pltpu.matmul_acc_lhs(accs[m][r], tile(sep_now, m, r), load_staged_rhs=0 if r == 0 else None)
        push()
        for j in range(4):
            for q in range(4):
                sep_now[j, q] = sep_next[j, q]
        sep, ang = geometry(state)
        put(sep_next, sep)
        put(ang_next, ang)
        return advance(state)

    lax.fori_loop(0, total, turn, advance(second))

    sums = []
    for m in range(2):
        pltpu.matmul_acc_lhs(accs[m][0], jnp.zeros((SPAN, 2 * LANES), jnp.float32), load_staged_rhs=0)
    out = None
    for r in range(SLOTS):
        got = pltpu.matmul_pop(accs[0][r]) + pltpu.matmul_pop(accs[1][r])
        side = r * SPAN // LANES
        got = got[:, side * LANES:(side + 1) * LANES]
        shift = (r * SPAN) % LANES
        if shift:
            got = pltpu.roll(got, LANES - shift, 1)
        out = got if out is None else out + got
    lane = lax.broadcasted_iota(jnp.int32, (SPAN, LANES), 1)
    from_lane = jnp.where(lane % 2 == 0, lane // 2, 16 + lane // 2) % LANES
    out = jnp.take_along_axis(out, from_lane, axis=1) * (4.0 * out_scale)
    half = SBINS // 2
    out_ref[pl.ds(0, half, stride=2), :] = out[:half, :MUBINS]
    out_ref[pl.ds(1, half, stride=2), :] = out[16:16 + half, :MUBINS]


def passed_along(shard, axis, by):
    count = lax.axis_size(axis)
    return lax.ppermute(shard, axis, [(i, (i + by) % count) for i in range(count)])


def swapped(shard, axis, mask):
    return lax.ppermute(shard, axis, [(i, i ^ mask) for i in range(lax.axis_size(axis))])


def per_device(positions, weights, block_count, send_list, unit_pair, unit_live):
    blocks, _, block = positions.shape
    per_peer = send_list.shape[2]
    peers = lax.axis_size("wa")
    units = peers * per_peer
    smem = pl.BlockSpec(memory_space=pltpu.SMEM)
    vmem = pl.BlockSpec(memory_space=pltpu.VMEM)
    slot = jax.ShapeDtypeStruct((units, 4, block), jnp.float32)
    payload = pl.pallas_call(
        pack_kernel, out_shape=slot, in_specs=[smem, smem, vmem, vmem], out_specs=vmem, name="pack"
    )(block_count, send_list, positions, weights)
    own = lax.all_to_all(payload, "wa", split_axis=0, concat_axis=0, tiled=True)
    below = passed_along(own, "gx", 1)
    scale = 10.0 * SBINS * MUBINS / (peers * units * block * block)
    held = pltpu.VMEM((4, 4, ROWS, LANES), jnp.float32)

    def outer(*refs):
        def inner(*accs):
            pair_kernel(scale, *refs, *accs)

        pl.run_scoped(inner, *[pltpu.ACC(m)((SPAN, 2 * LANES), jnp.float32) for m in range(2) for _ in range(SLOTS)])

    total = pl.pallas_call(
        outer,
        out_shape=jax.ShapeDtypeStruct((SBINS, MUBINS), jnp.float32),
        in_specs=[smem, smem, vmem, vmem],
        out_specs=vmem,
        scratch_shapes=[
            pltpu.VMEM((2 * units, block // LANES, 8, LANES), jnp.float32),
            pltpu.VMEM((2 * units, block, 8), jnp.float32),
            held, held, held,
            pltpu.SMEM((units,), jnp.int32),
            pltpu.SMEM((2 * units,), jnp.int32),
            pltpu.SMEM((units,), jnp.int32),
            pltpu.SMEM((units,), jnp.int32),
        ],
        name="pairs",
    )(unit_live, unit_pair, own, below)
    total = total + swapped(total, "wa", 1)
    slab = total
    for mask in range(2, peers, 2):
        slab = slab + swapped(total, "wa", mask)
    whole = slab
    for by in range(1, lax.axis_size("gx")):
        whole = whole + passed_along(slab, "gx", by)
    return (slab[None], whole / lax.axis_size("gx"))


def solution(mesh):
    return jax.shard_map(
        per_device,
        mesh=mesh,
        in_specs=(
            P(("gx", "wa"), None, None),
            P(("gx", "wa"), None),
            P(("gx", "wa")),
            P(("gx", "wa"), None, None),
            P(("gx", "wa"), None),
            P(("gx", "wa")),
        ),
        out_specs=(P("gx", None, None), P()),
        check_vma=False,
    )
```

time: 133 us -> 53.9 us (0.41)
  matrix products: 47.8 us -> 0 us
  blocking collectives: 39.5 us -> 10.2 us
  Pallas kernels: 0 us -> 18.8 us
  other arithmetic: 11.2 us -> 0.74 us
  local copies, waits for them, and re-layouts: 11.3 us -> 4.79 us
  starting transfers between devices: 11.7 us -> 7.09 us
  waiting for transfers between devices: 8.92 us -> 10.9 us
    dot_general x4 -> x0, matrix products: 47.8 us -> none  [group_counts(): jnp.einsum('gkab,gjab->kj', s_hat, m_hat, preferred_element_type=jnp.floa...]
    psum x2 -> x0, blocking collectives: 39.5 us -> none  [the longest x1 22.3 us: per_device(): slab = lax.psum(total, 'wa') * scale]
    pallas_call x0 -> x2, Pallas kernels: none -> 18.8 us  [the longest x1 17.2 us: per_device(): pl.pallas_call(outer, out_shape=jax.ShapeDtypeStruct((SBINS, MUBINS), jnp...]
    all_to_all x0 -> x1, blocking collectives: none -> 10.2 us  [per_device(): own = lax.all_to_all(payload, 'wa', split_axis=0, concat_axis=0, tiled=True)]
    all_to_all x2 -> x0, starting transfers between devices: 8.54 us -> none  [the longest x1 5.2 us: per_device(): lax.all_to_all(send_wgt, 'wa', split_axis=0, concat_axis=0, tiled=True)]
    reduce_sum x4 -> x0, other arithmetic: 5.74 us -> none  [group_counts(): jnp.sum(diff * middle, axis=1)]
    all_to_all x2 -> x0, waiting for transfers between devices: 5.32 us -> none  [the longest x1 3.19 us: per_device(): lax.all_to_all(send_pos, 'wa', split_axis=0, concat_axis=0, tiled=True)]
    ppermute x2 -> x4, waiting for transfers between devices: 3.6 us -> 7.81 us  [passed_along(): lax.ppermute(shard, axis, [(i, (i + by) % count) for i in range(count)])]
  transfers between devices with their start and end apart: 4 -> 8, of which waited for: 3 -> 7; matrix products, arithmetic and copies ran while one was open for 2% -> 1% of each run, Pallas kernels for 0% -> 0%
where the time goes in v1:
time: 53.9 us; the launch traced here: 53.8 us
  Pallas kernels  18.8 us (35%)
  waiting for transfers between devices  10.9 us (20%)
  blocking collectives  10.2 us (19%)
  starting transfers between devices  7.09 us (13%)
  local copies, waits for them, and re-layouts  4.79 us (9%)
  between operations  1.3 us (2%)
  other arithmetic  0.74 us (1%)
    pallas_call x1, Pallas kernels, per_device(): pl.pallas_call(outer, out_shape=jax.ShapeDtypeStruct((SBINS, MUBINS), jnp...  17.2 us
    all_to_all x1, blocking collectives, per_device(): own = lax.all_to_all(payload, 'wa', split_axis=0, concat_axis=0, tiled=True)  10.2 us
    ppermute x4, waiting for transfers between devices, passed_along(): lax.ppermute(shard, axis, [(i, (i + by) % count) for i in range(count)])  7.81 us
    unnamed x8, local copies, waits for them, and re-layouts  4.79 us
    ppermute x4, starting transfers between devices, passed_along(): lax.ppermute(shard, axis, [(i, (i + by) % count) for i in range(count)])  3.6 us
    ppermute x4, starting transfers between devices, swapped(): lax.ppermute(shard, axis, [(i, i ^ mask) for i in range(lax.axis_size(axi...  3.49 us
    ppermute x4, waiting for transfers between devices, swapped(): lax.ppermute(shard, axis, [(i, i ^ mask) for i in range(lax.axis_size(axi...  3.11 us
    pallas_call x1, Pallas kernels, per_device(): pl.pallas_call(pack_kernel, out_shape=slot, in_specs=[smem, smem, vmem, v...  1.54 us
  transfers between devices with their start and end apart: 8, of which 7 were waited for; matrix products, arithmetic and copies ran while one was open for 1% of the time, Pallas kernels for 0%

profile of v1, /device:TPU:0, one launch (start us, length us, event | category | flops | bytes accessed | tf_op | source)
XLA Modules:
  0.0 53.8 jit_solution(3351821164410599061)
XLA Ops:
  0.6 1.3 %copy.8.send_ref = s32[1,8,2]{2,1,0:T(8,128)} copy(s32[1,8,2]{1,2,0:T(2,128)} %param.9) | data formatting | bytes 128 | tf_op args[3]
  2.0 1.5 %copy.9.pos_ref = f32[16,3,256]{2,1,0:T(4,128)} copy(f32[16,3,256]{2,0,1:T(8,128)} %param.6) | data formatting | bytes 98304 | tf_op args[0]
  3.4 1.5 %pack.1 = f32[16,4,256]{2,1,0:T(4,128)} custom-call(s32[16]{0:T(128)} %count_ref.1, s32[1,8,2]{2,1,0:T(8,128)} %copy.8.send_ref, f32[16,3,256]{2,1,0:T(4,128)} %copy.9.pos_ref, f32[16,256]{1,0:T(8,128)} %wgt_ref.1), custom_call_target="tpu_custom_call" | custom-call | tf_op jit(solution)/shard_map/pack/pallas_call | solution.py:211
  5.0 10.2 %all_to_all.5.refs_2_ = f32[16,4,256]{2,1,0:T(4,128)S(1)} all-to-all(f32[16,4,256]{2,1,0:T(4,128)} %pack.1), channel_id=1, replica_groups=mesh['gx'=4,'wa'=8] {'wa'}, dimensions={0} | all-to-all | bytes 131072 | tf_op jit(solution)/shard_map/all_to_all | solution.py:214
  15.2 0.0 copy-start
  15.2 1.6 %collective-permute-start = (f32[16,4,256]{2,1,0:T(4,128)S(1)}, f32[16,4,256]{2,1,0:T(4,128)S(1)}, u32[]{:S(2)}, u32[]{:S(2)}) collective-permute-start(f32[16,4,256]{2,1,0:T(4,128)S(1)} %all_to_all.5.refs_2_), channel_id=1, source_target_pairs={{0,8},{8,16},{16,24},{24,0},{1,9},{9,17},{17,25},{25,1},{2,10},{10... | collective-permute-start | bytes 196616 | tf_op jit(solution)/shard_map/ppermute | solution.py:196
  17.4 3.8 %collective-permute-done.refs_3_ = f32[16,4,256]{2,1,0:T(4,128)S(1)} collective-permute-done((f32[16,4,256]{2,1,0:T(4,128)S(1)}, f32[16,4,256]{2,1,0:T(4,128)S(1)}, u32[]{:S(2)}, u32[]{:S(2)}) %collective-permute-start) | collective-permute-done | bytes 65568 | tf_op jit(solution)/shard_map/ppermute | solution.py:196
  21.3 0.0 copy-done
  21.3 0.0 copy-start.1
  21.3 0.6 %copy-done.1 = f32[16,4,256]{2,1,0:T(4,128)} copy-done((f32[16,4,256]{2,1,0:T(4,128)}, f32[16,4,256]{2,1,0:T(4,128)S(1)}, u32[]{:S(2)}) %copy-start.1) | copy-done | bytes 65560
  21.9 17.2 %pairs.1 = f32[30,20]{1,0:T(8,128)} custom-call(s32[1]{0:T(128)S(6)} %copy.12.refs_0_, s32[1,16]{1,0:T(1,128)} %refs_1_.1, f32[16,4,256]{2,1,0:T(4,128)} %copy-done, f32[16,4,256]{2,1,0:T(4,128)} %copy-done.1), custom_call_target="tpu_custom_call" | custom-call | tf_op jit(solution)/shard_map/pairs/pallas_call | solution.py:225
  39.1 0.0 collective-permute-start.1
  39.1 1.4 %collective-permute-done.1 = f32[30,20]{1,0:T(8,128)S(1)} collective-permute-done((f32[30,20]{1,0:T(8,128)}, f32[30,20]{1,0:T(8,128)S(1)}, u32[]{:S(2)}, u32[]{:S(2)}) %collective-permute-start.1) | collective-permute-done | bytes 2432 | tf_op jit(solution)/shard_map/ppermute | solution.py:200
  40.5 0.7 %add.21 = f32[30,20]{1,0:T(8,128)S(1)} add(f32[30,20]{1,0:T(8,128)} %pairs.1, f32[30,20]{1,0:T(8,128)S(1)} %collective-permute-done.1) | non-fusion elementwise | flops 600 | bytes 7200 | tf_op jit(solution)/shard_map/add | solution.py:241
  41.2 0.0 collective-permute-start.4
  41.2 0.0 collective-permute-start.3
  41.2 3.5 %collective-permute-start.2 = (f32[30,20]{1,0:T(8,128)S(1)}, f32[30,20]{1,0:T(8,128)S(1)}, u32[]{:S(2)}, u32[]{:S(2)}) collective-permute-start(f32[30,20]{1,0:T(8,128)S(1)} %add.21), channel_id=1, source_target_pairs={{0,2},{1,3},{2,0},{3,1},{4,6},{5,7},{6,4},{7,5},{8,10},{9,11},{10,... | collective-permute-start | bytes 7208 | tf_op jit(solution)/shard_map/ppermute | solution.py:200
  44.7 1.1 %collective-permute-done.4 = f32[30,20]{1,0:T(8,128)S(1)} collective-permute-done((f32[30,20]{1,0:T(8,128)S(1)}, f32[30,20]{1,0:T(8,128)S(1)}, u32[]{:S(2)}, u32[]{:S(2)}) %collective-permute-start.4) | collective-permute-done | bytes 2432 | tf_op jit(solution)/shard_map/ppermute | solution.py:200
  45.9 0.0 collective-permute-done.3
  45.9 0.6 %collective-permute-done.2 = f32[30,20]{1,0:T(8,128)S(1)} collective-permute-done((f32[30,20]{1,0:T(8,128)S(1)}, f32[30,20]{1,0:T(8,128)S(1)}, u32[]{:S(2)}, u32[]{:S(2)}) %collective-permute-start.2) | collective-permute-done | bytes 2432 | tf_op jit(solution)/shard_map/ppermute | solution.py:200
  46.4 1.1 %collective-permute-start.7 = (f32[30,20]{1,0:T(8,128)S(1)}, f32[30,20]{1,0:T(8,128)S(1)}, u32[]{:S(2)}, u32[]{:S(2)}) collective-permute-start(f32[30,20]{1,0:T(8,128)S(1)} %add_add_fusion), channel_id=1, source_target_pairs={{0,24},{8,0},{16,8},{24,16},{1,25},{9,1},{17,9},{25,17},{2,26},{10... | collective-permute-start | bytes 7208 | tf_op jit(solution)/shard_map/ppermute | solution.py:196
  47.6 0.0 collective-permute-start.6
  47.6 0.9 %collective-permute-start.5 = (f32[30,20]{1,0:T(8,128)S(1)}, f32[30,20]{1,0:T(8,128)S(1)}, u32[]{:S(2)}, u32[]{:S(2)}) collective-permute-start(f32[30,20]{1,0:T(8,128)S(1)} %add_add_fusion), channel_id=1, source_target_pairs={{0,8},{8,16},{16,24},{24,0},{1,9},{9,17},{17,25},{25,1},{2,10},{10... | collective-permute-start | bytes 7208 | tf_op jit(solution)/shard_map/ppermute | solution.py:196
  48.5 0.7 %copy.10 = f32[1,30,20]{1,0,2:T(1,128)} copy(f32[1,30,20]{2,1,0:T(8,128)S(1)} %bitcast.1) | data formatting | bytes 4800
  49.1 1.0 %collective-permute-done.7 = f32[30,20]{1,0:T(8,128)S(1)} collective-permute-done((f32[30,20]{1,0:T(8,128)S(1)}, f32[30,20]{1,0:T(8,128)S(1)}, u32[]{:S(2)}, u32[]{:S(2)}) %collective-permute-start.7) | collective-permute-done | bytes 2432 | tf_op jit(solution)/shard_map/ppermute | solution.py:196
  50.2 2.0 %collective-permute-done.6 = f32[30,20]{1,0:T(8,128)S(1)} collective-permute-done((f32[30,20]{1,0:T(8,128)S(1)}, f32[30,20]{1,0:T(8,128)S(1)}, u32[]{:S(2)}, u32[]{:S(2)}) %collective-permute-start.6) | collective-permute-done | bytes 2432 | tf_op jit(solution)/shard_map/ppermute | solution.py:196
  52.2 0.9 %collective-permute-done.5 = f32[30,20]{1,0:T(8,128)S(1)} collective-permute-done((f32[30,20]{1,0:T(8,128)S(1)}, f32[30,20]{1,0:T(8,128)S(1)}, u32[]{:S(2)}, u32[]{:S(2)}) %collective-permute-start.5) | collective-permute-done | bytes 2432 | tf_op jit(solution)/shard_map/ppermute | solution.py:196
  53.1 0.7 %copy.11 = f32[30,20]{0,1:T(8,128)} copy(f32[30,20]{1,0:T(8,128)S(1)} %add_multiply_fusion) | data formatting | bytes 4800
  (2 shorter events, 0.0 us)
Async XLA Ops:
  15.2 6.1 %copy-start = (f32[16,4,256]{2,1,0:T(4,128)}, f32[16,4,256]{2,1,0:T(4,128)S(1)}, u32[]{:S(2)}) copy-start(f32[16,4,256]{2,1,0:T(4,128)S(1)} %all_to_all.5.refs_2_) | copy-start | bytes 196612
  15.2 6.1 %collective-permute-start = (f32[16,4,256]{2,1,0:T(4,128)S(1)}, f32[16,4,256]{2,1,0:T(4,128)S(1)}, u32[]{:S(2)}, u32[]{:S(2)}) collective-permute-start(f32[16,4,256]{2,1,0:T(4,128)S(1)} %all_to_all.5.refs_2_), channel_id=1, source_target_pairs={{0,8},{8,16},{16,24},{24,0},{1,9},{9,17},{17,25},{25,1},{2,10},{10... | collective-permute-start | bytes 196616 | tf_op jit(solution)/shard_map/ppermute | solution.py:196
  21.3 0.6 %copy-start.1 = (f32[16,4,256]{2,1,0:T(4,128)}, f32[16,4,256]{2,1,0:T(4,128)S(1)}, u32[]{:S(2)}) copy-start(f32[16,4,256]{2,1,0:T(4,128)S(1)} %collective-permute-done.refs_3_) | copy-start | bytes 196612
  39.1 1.4 %collective-permute-start.1 = (f32[30,20]{1,0:T(8,128)}, f32[30,20]{1,0:T(8,128)S(1)}, u32[]{:S(2)}, u32[]{:S(2)}) collective-permute-start(f32[30,20]{1,0:T(8,128)} %pairs.1), channel_id=1, source_target_pairs={{0,1},{1,0},{2,3},{3,2},{4,5},{5,4},{6,7},{7,6},{8,9},{9,8},{10,11... | collective-permute-start | bytes 7208 | tf_op jit(solution)/shard_map/ppermute | solution.py:200
  41.2 4.6 %collective-permute-start.4 = (f32[30,20]{1,0:T(8,128)S(1)}, f32[30,20]{1,0:T(8,128)S(1)}, u32[]{:S(2)}, u32[]{:S(2)}) collective-permute-start(f32[30,20]{1,0:T(8,128)S(1)} %add.21), channel_id=1, source_target_pairs={{0,6},{1,7},{2,4},{3,5},{4,2},{5,3},{6,0},{7,1},{8,14},{9,15},{10,... | collective-permute-start | bytes 7208 | tf_op jit(solution)/shard_map/ppermute | solution.py:200
  41.2 4.6 %collective-permute-start.3 = (f32[30,20]{1,0:T(8,128)S(1)}, f32[30,20]{1,0:T(8,128)S(1)}, u32[]{:S(2)}, u32[]{:S(2)}) collective-permute-start(f32[30,20]{1,0:T(8,128)S(1)} %add.21), channel_id=1, source_target_pairs={{0,4},{1,5},{2,6},{3,7},{4,0},{5,1},{6,2},{7,3},{8,12},{9,13},{10,... | collective-permute-start | bytes 7208 | tf_op jit(solution)/shard_map/ppermute | solution.py:200
  41.2 5.2 %collective-permute-start.2 = (f32[30,20]{1,0:T(8,128)S(1)}, f32[30,20]{1,0:T(8,128)S(1)}, u32[]{:S(2)}, u32[]{:S(2)}) collective-permute-start(f32[30,20]{1,0:T(8,128)S(1)} %add.21), channel_id=1, source_target_pairs={{0,2},{1,3},{2,0},{3,1},{4,6},{5,7},{6,4},{7,5},{8,10},{9,11},{10,... | collective-permute-start | bytes 7208 | tf_op jit(solution)/shard_map/ppermute | solution.py:200
  46.4 3.7 %collective-permute-start.7 = (f32[30,20]{1,0:T(8,128)S(1)}, f32[30,20]{1,0:T(8,128)S(1)}, u32[]{:S(2)}, u32[]{:S(2)}) collective-permute-start(f32[30,20]{1,0:T(8,128)S(1)} %add_add_fusion), channel_id=1, source_target_pairs={{0,24},{8,0},{16,8},{24,16},{1,25},{9,1},{17,9},{25,17},{2,26},{10... | collective-permute-start | bytes 7208 | tf_op jit(solution)/shard_map/ppermute | solution.py:196
  47.6 4.6 %collective-permute-start.6 = (f32[30,20]{1,0:T(8,128)S(1)}, f32[30,20]{1,0:T(8,128)S(1)}, u32[]{:S(2)}, u32[]{:S(2)}) collective-permute-start(f32[30,20]{1,0:T(8,128)S(1)} %add_add_fusion), channel_id=1, source_target_pairs={{0,16},{8,24},{16,0},{24,8},{1,17},{9,25},{17,1},{25,9},{2,18},{10... | collective-permute-start | bytes 7208 | tf_op jit(solution)/shard_map/ppermute | solution.py:196
  47.6 5.5 %collective-permute-start.5 = (f32[30,20]{1,0:T(8,128)S(1)}, f32[30,20]{1,0:T(8,128)S(1)}, u32[]{:S(2)}, u32[]{:S(2)}) collective-permute-start(f32[30,20]{1,0:T(8,128)S(1)} %add_add_fusion), channel_id=1, source_target_pairs={{0,8},{8,16},{16,24},{24,0},{1,9},{9,17},{17,25},{25,1},{2,10},{10... | collective-permute-start | bytes 7208 | tf_op jit(solution)/shard_map/ppermute | solution.py:196
